TPU v7x, 32 devices: a whole 2x2x4 slice. The times are simulated.
32 devices in a mesh: expert: 4 (over x, core), ffn: 8 (over z, y).
Axes of the slice: x: 2, y: 2, z: 4, core: 2. Of those that a mesh axis runs over, the one named last changes fastest.
Arguments:
- tokens: bfloat16 [4, 32, 4096], P('expert', 'ffn'), may hold values from -6 to 6
- routes: int32 [4, 32, 2], P('expert'), may hold values from 0 to 3, all different within a row; in each aligned block of 32 rows (0 to 31, 32 to 63, ..., all dimensions but the last counted through in order) at most 24 rows name the same one
- router: bfloat16 [4096, 4], replicated, may hold values from -0.09375 to 0.09375
- w_gate: bfloat16 [4, 4096, 12288], P('expert', None, 'ffn'), may hold values from -0.09375 to 0.09375
- w_up: bfloat16 [4, 4096, 12288], P('expert', None, 'ffn'), may hold values from -0.09375 to 0.09375
- w_down: bfloat16 [4, 12288, 4096], P('expert', 'ffn'), may hold values from -0.078125 to 0.078125
- adapter: bfloat16 [4, 4096, 4096], P('expert', None, 'ffn'), may hold values from -0.09375 to 0.09375
- upstream: bfloat16 [4, 32, 4096], P('expert', None, 'ffn'), may hold values from -24 to 24
- bound: float32 [4], P('expert'), may hold values from 2048 to 16384
Outputs:
- adapted: bfloat16 [4, 32, 4096], P('expert', None, 'ffn')
- clipped: bfloat16 [4, 4096, 4096], P('expert', None, 'ffn')
Inputs may be any that keep to these rules, and one draw needn't show every extreme that they name: `routes`: each token names two different experts; for each client at most 24 of its tokens name any one expert, and in some clients some expert is named by exactly 24 tokens.
All inputs are finite; a program needn't handle non-finite values.
Results may differ from a plain program's by a relative error of at most 0.015.
Values may be sent and summed in bfloat16 or wider, within the bound.
A program may use at most 128 MiB of HBM per device.

v0:
```python
import jax
import jax.numpy as jnp
from jax import lax
from jax.sharding import PartitionSpec as P


def slot_table(routed, expert_count):
    named_hits = jnp.sum(
        (routed[:, :, None] == jnp.arange(expert_count, dtype=jnp.int32)[None, None, :]).astype(
            jnp.int32
        ),
        axis=1,
    )
    before = jnp.cumsum(named_hits, axis=0) - named_hits
    return jnp.take_along_axis(before, routed, axis=1)


def pack_rows(token_rows, routed, expert_count, capacity):
    token_count = token_rows.shape[0]
    slot_flat = routed * capacity + slot_table(routed, expert_count)
    owners = jnp.repeat(jnp.arange(token_count, dtype=jnp.int32), 2)
    source = (
        jnp.full((expert_count * capacity,), token_count, jnp.int32)
        .at[slot_flat.reshape(-1)]
        .set(owners)
    )
    padded = jnp.concatenate(
        [token_rows, jnp.zeros((1, token_rows.shape[1]), token_rows.dtype)], axis=0
    )
    return (padded[source].reshape(expert_count, capacity, token_rows.shape[1]), slot_flat)


def mix_weights(token_rows, routed, router):
    logits = jnp.dot(token_rows, router, preferred_element_type=jnp.float32)
    picked = jnp.take_along_axis(logits, routed, axis=1)
    weight_first = jax.nn.sigmoid(picked[:, 0] - picked[:, 1])
    return (weight_first, 1.0 - weight_first)


def per_device(tokens, routes, router, w_gate, w_up, w_down, adapter, upstream, bound):
    expert_count = lax.axis_size("expert")
    gathered = lax.all_gather(tokens, "ffn", axis=1, tiled=True)
    token_rows = gathered[0]
    token_count = token_rows.shape[0]
    model_width = token_rows.shape[1]
    capacity = 3 * token_count // expert_count
    routed = routes[0]
    outgoing, slot_flat = pack_rows(token_rows, routed, expert_count, capacity)
    col_count = adapter.shape[2]
    column = lax.axis_index("ffn") * col_count
    weight_first, weight_second = mix_weights(token_rows, routed, router)
    arrived = lax.all_to_all(outgoing, "expert", split_axis=0, concat_axis=0, tiled=True)
    flat_rows = arrived.reshape(-1, model_width)
    gate_out = jnp.dot(flat_rows, w_gate[0], preferred_element_type=jnp.float32)
    up_out = jnp.dot(flat_rows, w_up[0], preferred_element_type=jnp.float32)
    hidden = (jax.nn.silu(gate_out) * up_out).astype(jnp.bfloat16)
    down_piece = jnp.dot(hidden, w_down[0], preferred_element_type=jnp.float32).astype(jnp.bfloat16)
    returned = lax.all_to_all(
        down_piece.reshape(arrived.shape), "expert", split_axis=0, concat_axis=0, tiled=True
    )
    picked = returned.reshape(-1, model_width)[slot_flat]
    mix_share = weight_first[:, None] * picked[:, 0].astype(jnp.float32) + weight_second[
        :, None
    ] * picked[:, 1].astype(jnp.float32)
    mixture = lax.psum(mix_share, "ffn")
    layer_out = (token_rows.astype(jnp.float32) + mixture).astype(jnp.bfloat16)
    own_cols = lax.dynamic_slice_in_dim(layer_out, column, col_count, 1)
    adapted = (
        own_cols.astype(jnp.float32)
        + jnp.dot(layer_out, adapter[0], preferred_element_type=jnp.float32)
    ).astype(jnp.bfloat16)
    grad_input = upstream[0]
    adapter_grad = lax.dot_general(
        layer_out, grad_input, (((0,), (0,)), ((), ())), preferred_element_type=jnp.float32
    )
    cotangent_gram = lax.dot_general(
        grad_input, grad_input, (((1,), (1,)), ((), ())), preferred_element_type=jnp.float32
    )
    whole_gram = lax.psum(cotangent_gram, "ffn")
    layer_gram = lax.dot_general(
        layer_out, layer_out, (((1,), (1,)), ((), ())), preferred_element_type=jnp.float32
    )
    squared = jnp.sum(layer_gram * whole_gram)
    grad_norm = jnp.sqrt(squared)
    clip_limit = bound[0]
    factor = clip_limit / jnp.maximum(grad_norm, clip_limit)
    clipped = (adapter_grad * factor).astype(jnp.bfloat16)
    return (adapted[None], clipped[None])


def solution(mesh):
    in_specs = (
        P("expert", "ffn", None),
        P("expert", None, None),
        P(),
        P("expert", None, "ffn"),
        P("expert", None, "ffn"),
        P("expert", "ffn", None),
        P("expert", None, "ffn"),
        P("expert", None, "ffn"),
        P("expert"),
    )
    out_specs = (P("expert", None, "ffn"), P("expert", None, "ffn"))
    return jax.shard_map(
        per_device, mesh=mesh, in_specs=in_specs, out_specs=out_specs, check_vma=False
    )
```

profile of v0, /device:TPU:0, one launch (start us, length us, event | category | flops | bytes accessed | tf_op | source)
XLA Modules:
  0.0 190.7 jit_solution(15884546444229429780)
XLA Ops:
  7.2 0.7 shift-left_or_fusion
  7.9 0.8 copy.46
  8.6 0.7 convert_reduce_fusion
  9.5 0.1 reshape.206
  9.7 0.1 squeeze.35
  9.8 0.1 reshape.222
  9.9 0.8 gather_fusion.3
  10.7 0.8 scatter_custom_fusion
  11.6 33.0 %all_gather.3 = bf16[1,32,4096]{2,0,1:T(2,128)(2,1)S(1)} all-gather(bf16[1,4,4096]{2,0,1:T(2,128)(2,1)S(1)} %copy.43), channel_id=1, replica_groups=mesh['expert'=4,'ffn'=8] {'ffn'}, dimensions={1}, use_global_device_ids=true | all-gather | bytes 294912 | tf_op jit(solution)/shard_map/all_gather | solution.py:42
  44.6 0.3 copy.65
  45.0 1.9 %gather_fusion = bf16[96,4096]{1,0:T(8,128)(2,1)} fusion(bf16[33,4096]{1,0:T(8,128)(2,1)S(1)} %concatenate.3, s32[1024]{0:T(1024)S(1)} %pad_clamp_fusion.1), kind=kCustom, calls=%fused_computation | custom fusion | bytes 1573248 | tf_op jit(solution)/shard_map/gather | solution.py:30
  46.9 3.5 %all-to-all-start = ((bf16[4,24,4096]{2,1,0:T(8,128)(2,1)}), bf16[4,24,4096]{2,1,0:T(8,128)(2,1)S(1)}, u32[]{:S(2)}, u32[]{:S(2)}) async-start(bf16[4,24,4096]{2,1,0:T(8,128)(2,1)} %bitcast.5), calls=%async_computation | async-start | bytes 1572864 | tf_op jit(solution)/shard_map/all_to_all | solution.py:52
  50.6 0.2 fusion.43
  50.8 11.2 %all-to-all-done = bf16[4,24,4096]{2,1,0:T(8,128)(2,1)S(1)} async-done(((bf16[4,24,4096]{2,1,0:T(8,128)(2,1)}), bf16[4,24,4096]{2,1,0:T(8,128)(2,1)S(1)}, u32[]{:S(2)}, u32[]{:S(2)}) %all-to-all-start) | async-done | bytes 786464 | tf_op jit(solution)/shard_map/all_to_all | solution.py:52
  62.0 6.7 %fusion.4 = f32[96,1536]{1,0:T(8,128)S(1)} fusion(bf16[96,4096]{1,0:T(8,128)(2,1)S(1)} %bitcast.93, bf16[1,4096,1536]{2,1,0:T(8,128)(2,1)} %param.12), kind=kOutput, calls=%fused_computation.9 | convolution fusion | flops 1207959552 | bytes 13959168 | tf_op jit(solution)/shard_map/dot_general | solution.py:54
  68.7 13.3 %fusion.7 = bf16[96,4096]{1,0:T(8,128)(2,1)} fusion(bf16[1,1536,4096]{2,1,0:T(8,128)(2,1)} %param.14, bf16[96,4096]{1,0:T(8,128)(2,1)S(1)} %bitcast.94, bf16[1,4096,1536]{2,1,0:T(8,128)(2,1)} %param.13, f32[96,1536]{1,0:T(8,128)S(1)} %fusion.4), kind=kOutput, calls=%fused_computation.13 | convolution fusion | flops 2417197056 | bytes 27328512 | tf_op jit(solution)/shard_map/dot_general | solution.py:57
  82.0 3.5 %all-to-all-start.1 = ((bf16[4,24,4096]{2,1,0:T(8,128)(2,1)}), bf16[4,24,4096]{2,1,0:T(8,128)(2,1)S(1)}, u32[]{:S(2)}, u32[]{:S(2)}) async-start(bf16[4,24,4096]{2,1,0:T(8,128)(2,1)} %bitcast.10), calls=%async_computation.1 | async-start | bytes 1572864 | tf_op jit(solution)/shard_map/all_to_all | solution.py:58
  85.6 0.1 reshape.200
  85.7 0.9 gather_fusion.2
  86.6 0.1 reshape.209
  86.8 10.2 %all-to-all-done.1 = bf16[4,24,4096]{2,1,0:T(8,128)(2,1)S(1)} async-done(((bf16[4,24,4096]{2,1,0:T(8,128)(2,1)}), bf16[4,24,4096]{2,1,0:T(8,128)(2,1)S(1)}, u32[]{:S(2)}, u32[]{:S(2)}) %all-to-all-start.1) | async-done | bytes 786464 | tf_op jit(solution)/shard_map/all_to_all | solution.py:58
  97.0 0.9 gather_fusion.1
  97.9 0.3 reshape.199
  98.3 1.2 fusion.42
  99.4 1.4 fusion.31
  101.6 0.1 fusion.33
  101.7 37.4 %psum.15 = f32[32,32]{1,0:T(8,128)S(1)} all-reduce(f32[32,32]{1,0:T(8,128)S(1)} %fusion.33), channel_id=1, replica_groups=mesh['expert'=4,'ffn'=8] {'ffn'}, use_global_device_ids=true, to_apply=%region_4.5 | all-reduce | flops 1024 | bytes 8192 | tf_op jit(solution)/shard_map/psum | solution.py:79
  139.1 35.0 %all-reduce.3.cloned.1.call-done = f32[32,4096]{1,0:T(8,128)} async-done(((f32[32,4096]{1,0:T(8,128)}), f32[32,4096]{1,0:T(8,128)}) %all-reduce.3.cloned.1.call-update) | async-done | bytes 524304 | tf_op jit(solution)/shard_map/psum | solution.py:65
  174.1 1.4 add_convert_fusion
  175.4 0.8 fusion.30
  177.0 3.3 %fusion.6 = bf16[1,4096,512]{2,1,0:T(8,128)(2,1)} fusion(bf16[32,4096]{1,0:T(8,128)(2,1)S(1)} %add_convert_fusion, f32[]{:T(128)S(6)} %div.14, bf16[1,32,512]{2,1,0:T(8,128)(2,1)S(1)} %copy-done), kind=kOutput, calls=%fused_computation.12 | convolution fusion | flops 138412032 | bytes 4489220 | tf_op jit(solution)/shard_map/dot_general | solution.py:73
  180.2 3.6 %fusion.24 = bf16[1,32,512]{2,1,0:T(8,128)(2,1)} fusion(bf16[32,4096]{1,0:T(8,128)(2,1)S(1)} %add_convert_fusion, bf16[1,4096,512]{2,1,0:T(8,128)(2,1)} %param.15, s32[]{:T(128)S(6)} %select_n.91), kind=kOutput, calls=%fused_computation.20 | convolution fusion | flops 134266880 | bytes 4521988 | tf_op jit(solution)/shard_map/dot_general | solution.py:70
  (28 shorter events, 0.8 us)
Async XLA Ops:
  7.2 94.4 %copy-start = (bf16[1,32,512]{2,1,0:T(8,128)(2,1)S(1)}, bf16[1,32,512]{2,1,0:T(8,128)(2,1)}, u32[]{:S(2)}) copy-start(bf16[1,32,512]{2,1,0:T(8,128)(2,1)} %param.16) | copy-start | bytes 98308
  7.2 4.4 %copy-start.1 = (bf16[1,4,4096]{2,1,0:T(4,128)(2,1)S(1)}, bf16[1,4,4096]{2,1,0:T(4,128)(2,1)}, u32[]{:S(2)}) copy-start(bf16[1,4,4096]{2,1,0:T(4,128)(2,1)} %param.9) | copy-start | bytes 98308
  9.9 40.7 %copy-start.3 = (bf16[4096,4]{0,1:T(4,128)(2,1)S(1)}, bf16[4096,4]{0,1:T(4,128)(2,1)}, u32[]{:S(2)}) copy-start(bf16[4096,4]{0,1:T(4,128)(2,1)} %param.11) | copy-start | bytes 98308
  46.9 15.1 %all-to-all-start = ((bf16[4,24,4096]{2,1,0:T(8,128)(2,1)}), bf16[4,24,4096]{2,1,0:T(8,128)(2,1)S(1)}, u32[]{:S(2)}, u32[]{:S(2)}) async-start(bf16[4,24,4096]{2,1,0:T(8,128)(2,1)} %bitcast.5), calls=%async_computation | async-start | bytes 1572864 | tf_op jit(solution)/shard_map/all_to_all | solution.py:52
  68.6 16.9 %copy-start.2 = (s32[1,32,2]{1,2,0:T(2,128)S(1)}, s32[1,32,2]{1,2,0:T(2,128)}, u32[]{:S(2)}) copy-start(s32[1,32,2]{1,2,0:T(2,128)} %param.10) | copy-start | bytes 772
  82.0 15.1 %all-to-all-start.1 = ((bf16[4,24,4096]{2,1,0:T(8,128)(2,1)}), bf16[4,24,4096]{2,1,0:T(8,128)(2,1)S(1)}, u32[]{:S(2)}, u32[]{:S(2)}) async-start(bf16[4,24,4096]{2,1,0:T(8,128)(2,1)} %bitcast.10), calls=%async_computation.1 | async-start | bytes 1572864 | tf_op jit(solution)/shard_map/all_to_all | solution.py:58
  85.5 88.6 %all-reduce.3.cloned.1.call-start = ((), (), s32[]{:S(2)}) async-start(), calls=%async_computation.2 | async-start | bytes 1048576 | tf_op jit(solution)/shard_map/psum | solution.py:65
Sparse Core Ops, SparseCore 0:
  101.0 72.9 all-reduce.2
where the time goes:
time: 191 us
  blocking collectives  70.4 us (37%)
  waiting for transfers between devices  56.4 us (30%)
  matrix products  28 us (15%)
  between operations  15.6 us (8%)
  local copies, waits for them, and re-layouts  8.92 us (5%)
  starting transfers between devices  7.03 us (4%)
  other arithmetic  4.31 us (2%)
    psum x1, blocking collectives, per_device(): whole_gram = lax.psum(cotangent_gram, 'ffn')  37.4 us
    psum x1, waiting for transfers between devices, per_device(): mixture = lax.psum(mix_share, 'ffn')  35 us
    all_gather x1, blocking collectives, per_device(): gathered = lax.all_gather(tokens, 'ffn', axis=1, tiled=True)  33 us
    dot_general x1, matrix products, per_device(): jnp.dot(hidden, w_down[0], preferred_element_type=jnp.float32)  13.3 us
    all_to_all x1, waiting for transfers between devices, per_device(): lax.all_to_all(outgoing, 'expert', split_axis=0, concat_axis=0, tiled=True)  11.2 us
    all_to_all x1, waiting for transfers between devices, per_device(): lax.all_to_all(down_piece.reshape(arrived.shape), 'expert', split_axis=0,...  10.2 us
    dot_general x1, matrix products, per_device(): gate_out = jnp.dot(flat_rows, w_gate[0], preferred_element_type=jnp.float32)  6.66 us
  transfers between devices with their start and end apart: 3, of which 3 were waited for; matrix products, arithmetic and copies ran while one was open for 1% of the time, Pallas kernels for 0%

commit v1 on v0

--- a/solution.py
+++ b/solution.py
@@ -39,7 +39,7 @@
 
 def per_device(tokens, routes, router, w_gate, w_up, w_down, adapter, upstream, bound):
     expert_count = lax.axis_size("expert")
-    gathered = lax.all_gather(tokens, "ffn", axis=1, tiled=True)
+    gathered = jnp.concatenate(jax.lax.all_gather(tokens, axis_name="ffn"), 1)
     token_rows = gathered[0]
     token_count = token_rows.shape[0]
     model_width = token_rows.shape[1]

time: 191 us -> 190 us (level)
  no operation moved by 1% of the time
where the time goes in v1:
time: 190 us
  blocking collectives  69.8 us (37%)
  waiting for transfers between devices  56.5 us (30%)
  matrix products  28 us (15%)
  between operations  15.6 us (8%)
  local copies, waits for them, and re-layouts  8.63 us (5%)
  starting transfers between devices  7.03 us (4%)
  other arithmetic  4.06 us (2%)
    psum x1, blocking collectives, per_device(): whole_gram = lax.psum(cotangent_gram, 'ffn')  37.3 us
    psum x1, waiting for transfers between devices, per_device(): mixture = lax.psum(mix_share, 'ffn')  35 us
    all_gather x1, blocking collectives, per_device(): gathered = jnp.concatenate(jax.lax.all_gather(tokens, axis_name='ffn'), 1)  32.6 us
    dot_general x1, matrix products, per_device(): jnp.dot(hidden, w_down[0], preferred_element_type=jnp.float32)  13.3 us
    all_to_all x1, waiting for transfers between devices, per_device(): lax.all_to_all(outgoing, 'expert', split_axis=0, concat_axis=0, tiled=True)  11.2 us
    all_to_all x1, waiting for transfers between devices, per_device(): lax.all_to_all(down_piece.reshape(arrived.shape), 'expert', split_axis=0,...  10.2 us
    dot_general x1, matrix products, per_device(): gate_out = jnp.dot(flat_rows, w_gate[0], preferred_element_type=jnp.float32)  6.66 us
  transfers between devices with their start and end apart: 3, of which 3 were waited for; matrix products, arithmetic and copies ran while one was open for 1% of the time, Pallas kernels for 0%

profile of v1, /device:TPU:0, one launch (start us, length us, event | category | flops | bytes accessed | tf_op | source)
XLA Modules:
  0.0 189.6 jit_solution(5550533679147058522)
XLA Ops:
  7.2 0.7 shift-left_or_fusion
  7.9 0.8 copy.35
  8.6 0.7 convert_reduce_fusion
  9.5 0.1 reshape.206
  9.7 0.1 squeeze.31
  9.8 0.1 reshape.222
  9.9 0.8 gather_fusion.3
  10.7 0.8 scatter_custom_fusion
  11.6 32.6 %all-gather = bf16[8,4,4096]{2,1,0:T(4,128)(2,1)S(1)} all-gather(bf16[1,4,4096]{2,1,0:T(4,128)(2,1)S(1)} %copy-done.1), channel_id=2, replica_groups=mesh['expert'=4,'ffn'=8] {'ffn'}, dimensions={0}, use_global_device_ids=true | all-gather | bytes 294912 | tf_op jit(solution)/shard_map/all_gather | solution.py:42
  44.2 1.9 %gather_fusion = bf16[96,4096]{1,0:T(8,128)(2,1)} fusion(bf16[33,4096]{1,0:T(8,128)(2,1)S(1)} %concatenate.3, s32[1024]{0:T(1024)S(1)} %pad_clamp_fusion.1), kind=kCustom, calls=%fused_computation | custom fusion | bytes 1573248 | tf_op jit(solution)/shard_map/gather | solution.py:30
  46.1 3.5 %all-to-all-start = ((bf16[4,24,4096]{2,1,0:T(8,128)(2,1)}), bf16[4,24,4096]{2,1,0:T(8,128)(2,1)S(1)}, u32[]{:S(2)}, u32[]{:S(2)}) async-start(bf16[4,24,4096]{2,1,0:T(8,128)(2,1)} %bitcast.5), calls=%async_computation | async-start | bytes 1572864 | tf_op jit(solution)/shard_map/all_to_all | solution.py:52
  49.6 0.1 gather.22
  49.8 0.2 fusion.43
  50.0 11.2 %all-to-all-done = bf16[4,24,4096]{2,1,0:T(8,128)(2,1)S(1)} async-done(((bf16[4,24,4096]{2,1,0:T(8,128)(2,1)}), bf16[4,24,4096]{2,1,0:T(8,128)(2,1)S(1)}, u32[]{:S(2)}, u32[]{:S(2)}) %all-to-all-start) | async-done | bytes 786464 | tf_op jit(solution)/shard_map/all_to_all | solution.py:52
  61.2 6.7 %fusion.4 = f32[96,1536]{1,0:T(8,128)S(1)} fusion(bf16[96,4096]{1,0:T(8,128)(2,1)S(1)} %bitcast.88, bf16[1,4096,1536]{2,1,0:T(8,128)(2,1)} %param.12), kind=kOutput, calls=%fused_computation.9 | convolution fusion | flops 1207959552 | bytes 13959168 | tf_op jit(solution)/shard_map/dot_general | solution.py:54
  67.9 13.3 %fusion.7 = bf16[96,4096]{1,0:T(8,128)(2,1)} fusion(bf16[1,1536,4096]{2,1,0:T(8,128)(2,1)} %param.14, bf16[96,4096]{1,0:T(8,128)(2,1)S(1)} %bitcast.89, bf16[1,4096,1536]{2,1,0:T(8,128)(2,1)} %param.13, f32[96,1536]{1,0:T(8,128)S(1)} %fusion.4), kind=kOutput, calls=%fused_computation.13 | convolution fusion | flops 2417197056 | bytes 27328512 | tf_op jit(solution)/shard_map/dot_general | solution.py:57
  81.2 3.5 %all-to-all-start.1 = ((bf16[4,24,4096]{2,1,0:T(8,128)(2,1)}), bf16[4,24,4096]{2,1,0:T(8,128)(2,1)S(1)}, u32[]{:S(2)}, u32[]{:S(2)}) async-start(bf16[4,24,4096]{2,1,0:T(8,128)(2,1)} %bitcast.10), calls=%async_computation.1 | async-start | bytes 1572864 | tf_op jit(solution)/shard_map/all_to_all | solution.py:58
  84.9 0.1 reshape.200
  85.0 0.9 gather_fusion.2
  85.8 0.1 reshape.209
  86.1 10.2 %all-to-all-done.1 = bf16[4,24,4096]{2,1,0:T(8,128)(2,1)S(1)} async-done(((bf16[4,24,4096]{2,1,0:T(8,128)(2,1)}), bf16[4,24,4096]{2,1,0:T(8,128)(2,1)S(1)}, u32[]{:S(2)}, u32[]{:S(2)}) %all-to-all-start.1) | async-done | bytes 786464 | tf_op jit(solution)/shard_map/all_to_all | solution.py:58
  96.3 0.9 gather_fusion.1
  97.2 0.3 reshape.199
  97.5 1.2 fusion.42
  98.7 1.4 fusion.31
  100.8 0.1 fusion.33
  100.9 37.3 %psum.15 = f32[32,32]{1,0:T(8,128)S(1)} all-reduce(f32[32,32]{1,0:T(8,128)S(1)} %fusion.33), channel_id=1, replica_groups=mesh['expert'=4,'ffn'=8] {'ffn'}, use_global_device_ids=true, to_apply=%region_4.5 | all-reduce | flops 1024 | bytes 8192 | tf_op jit(solution)/shard_map/psum | solution.py:79
  138.2 35.0 %all-reduce.3.cloned.1.call-done = f32[32,4096]{1,0:T(8,128)} async-done(((f32[32,4096]{1,0:T(8,128)}), f32[32,4096]{1,0:T(8,128)}) %all-reduce.3.cloned.1.call-update) | async-done | bytes 524304 | tf_op jit(solution)/shard_map/psum | solution.py:65
  173.2 1.1 add_convert_fusion
  174.3 0.8 fusion.30
  175.8 3.3 %fusion.6 = bf16[1,4096,512]{2,1,0:T(8,128)(2,1)} fusion(bf16[32,4096]{1,0:T(8,128)(2,1)S(1)} %add_convert_fusion, f32[]{:T(128)S(6)} %div.14, bf16[1,32,512]{2,1,0:T(8,128)(2,1)S(1)} %copy-done), kind=kOutput, calls=%fused_computation.12 | convolution fusion | flops 138412032 | bytes 4489220 | tf_op jit(solution)/shard_map/dot_general | solution.py:73
  179.1 3.6 %fusion.24 = bf16[1,32,512]{2,1,0:T(8,128)(2,1)} fusion(bf16[32,4096]{1,0:T(8,128)(2,1)S(1)} %add_convert_fusion, bf16[1,4096,512]{2,1,0:T(8,128)(2,1)} %param.15, s32[]{:T(128)S(6)} %select_n.91), kind=kOutput, calls=%fused_computation.20 | convolution fusion | flops 134266880 | bytes 4521988 | tf_op jit(solution)/shard_map/dot_general | solution.py:70
  (27 shorter events, 0.7 us)
Async XLA Ops:
  7.2 93.6 %copy-start = (bf16[1,32,512]{2,1,0:T(8,128)(2,1)S(1)}, bf16[1,32,512]{2,1,0:T(8,128)(2,1)}, u32[]{:S(2)}) copy-start(bf16[1,32,512]{2,1,0:T(8,128)(2,1)} %param.16) | copy-start | bytes 98308
  7.2 4.4 %copy-start.1 = (bf16[1,4,4096]{2,1,0:T(4,128)(2,1)S(1)}, bf16[1,4,4096]{2,1,0:T(4,128)(2,1)}, u32[]{:S(2)}) copy-start(bf16[1,4,4096]{2,1,0:T(4,128)(2,1)} %param.9) | copy-start | bytes 98308
  9.9 39.9 %copy-start.3 = (bf16[4096,4]{0,1:T(4,128)(2,1)S(1)}, bf16[4096,4]{0,1:T(4,128)(2,1)}, u32[]{:S(2)}) copy-start(bf16[4096,4]{0,1:T(4,128)(2,1)} %param.11) | copy-start | bytes 98308
  46.1 15.1 %all-to-all-start = ((bf16[4,24,4096]{2,1,0:T(8,128)(2,1)}), bf16[4,24,4096]{2,1,0:T(8,128)(2,1)S(1)}, u32[]{:S(2)}, u32[]{:S(2)}) async-start(bf16[4,24,4096]{2,1,0:T(8,128)(2,1)} %bitcast.5), calls=%async_computation | async-start | bytes 1572864 | tf_op jit(solution)/shard_map/all_to_all | solution.py:52
  67.9 16.9 %copy-start.2 = (s32[1,32,2]{1,2,0:T(2,128)S(1)}, s32[1,32,2]{1,2,0:T(2,128)}, u32[]{:S(2)}) copy-start(s32[1,32,2]{1,2,0:T(2,128)} %param.10) | copy-start | bytes 772
  81.2 15.1 %all-to-all-start.1 = ((bf16[4,24,4096]{2,1,0:T(8,128)(2,1)}), bf16[4,24,4096]{2,1,0:T(8,128)(2,1)S(1)}, u32[]{:S(2)}, u32[]{:S(2)}) async-start(bf16[4,24,4096]{2,1,0:T(8,128)(2,1)} %bitcast.10), calls=%async_computation.1 | async-start | bytes 1572864 | tf_op jit(solution)/shard_map/all_to_all | solution.py:58
  84.7 88.5 %all-reduce.3.cloned.1.call-start = ((), (), s32[]{:S(2)}) async-start(), calls=%async_computation.2 | async-start | bytes 1048576 | tf_op jit(solution)/shard_map/psum | solution.py:65
Sparse Core Ops, SparseCore 0:
  100.3 72.8 all-reduce.2
